TPU v7x, 64 devices: a 2x2x8 block of a 4x4x8 slice. The times are simulated.
64 devices in a mesh: prob: 4 (over x, y), feat: 16 (over z, core).
Axes of the slice: x: 2, y: 2, z: 8, core: 2. Of those that a mesh axis runs over, the one named last changes fastest.
The devices are a block of a 4x4x8 slice.
Arguments:
- design: bfloat16 [16384, 32768], P('prob', 'feat'), parts along dimension 0
- targets: float32 [16384, 300], P('prob'), parts along dimension 0
- weights_init: float32 [131072, 300], P(('prob', 'feat')), parts along dimension 0
- step_sizes: float32 [131072], P(('prob', 'feat')), parts along dimension 0
Outputs:
- output 1: float32 [131072, 300], P(('prob', 'feat')), parts along dimension 0
- output 2: float32 [16384, 300], P('prob'), parts along dimension 0
There are 4 independent parts. A program takes and returns all parts, laid end to end along the dimension named above; each array names one.
All inputs are finite; a program needn't handle non-finite values.
Results may differ from a plain program's by a relative error of at most 0.001.
Values are sent between devices in bfloat16 or wider.
A program may use at most 768 MiB of HBM per device.

v0:
```python
import jax
import jax.numpy as jnp
from jax import lax
from jax.sharding import PartitionSpec as P, NamedSharding

SWEEPS = 6
RIDGE_COEF = 1.0
MIX_WEIGHT = 0.75


def solution(mesh):
    def local_solve(design, targets, weights, step_sizes):
        samples = design.shape[0]
        ridge_val = RIDGE_COEF / samples
        step_col = step_sizes[:, None]
        partial = jnp.dot(design, weights.astype(jnp.bfloat16), preferred_element_type=jnp.float32)
        residual = targets - lax.psum(partial, 'feat')
        for _ in range(SWEEPS):
            gradient = lax.dot_general(design, residual.astype(jnp.bfloat16), (((0,), (0,)), ((), ())), preferred_element_type=jnp.float32) / samples
            update = step_col * (gradient - ridge_val * weights)
            weights = weights + MIX_WEIGHT * update
            contrib = jnp.dot(design, update.astype(jnp.bfloat16), preferred_element_type=jnp.float32)
            residual = residual - MIX_WEIGHT * lax.psum(contrib, 'feat')
        return weights, residual

    return jax.shard_map(
        local_solve,
        mesh=mesh,
        in_specs=(P('prob', 'feat'), P('prob', None), P(('prob', 'feat'), None), P(('prob', 'feat'))),
        out_specs=(P(('prob', 'feat'), None), P('prob', None)),
        check_vma=False,
    )
```

profile of v0, /device:TPU:21, one launch (start us, length us, event | category | flops | bytes accessed | tf_op | source)
XLA Modules:
  0.0 1083.7 jit_solution(10385888767399177263)
XLA Ops:
  7.2 19.0 %fusion.30 = f32[4096,300]{0,1:T(8,128)} fusion(bf16[4096,2048]{1,0:T(8,128)(2,1)} %param.4, f32[2048,300]{0,1:T(8,128)} %param.6), kind=kOutput, calls=%fused_computation.54 | convolution fusion | flops 5033779200 | bytes 24150016 | tf_op jit(solution)/shard_map/dot_general | solution.py:16
  26.4 121.5 %all-reduce.8.cloned.1.call-done = f32[4096,300]{0,1:T(8,128)} async-done(((f32[4096,300]{0,1:T(8,128)}), f32[4096,300]{0,1:T(8,128)}) %all-reduce.8.cloned.1.call-update) | async-done | bytes 4915216 | tf_op jit(solution)/shard_map/psum | solution.py:17
  147.9 4.7 sub.39
  152.6 2.3 copy-done.2
  154.8 10.8 fusion.17
  165.6 19.1 %convolution_bitcast_fusion.5 = f32[4096,300]{0,1:T(8,128)} fusion(bf16[4096,2048]{1,0:T(8,128)(2,1)} %param.4, f32[2048,300]{0,1:T(8,128)} %fusion.17), kind=kOutput, calls=%fused_computation.5 | convolution fusion | flops 5033779200 | bytes 24150016 | tf_op jit(solution)/shard_map/dot_general | solution.py:22
  184.8 0.3 all-reduce.12.cloned.1.call-start
  185.0 117.4 %all-reduce.10.cloned.1.call-done = f32[4096,300]{0,1:T(8,128)} async-done(((f32[4096,300]{0,1:T(8,128)}), f32[4096,300]{0,1:T(8,128)}) %all-reduce.10.cloned.1.call-update) | async-done | bytes 4915216 | tf_op jit(solution)/shard_map/psum | solution.py:23
  302.4 13.7 %multiply_add_fusion.4 = (f32[2048,300]{0,1:T(8,128)}, bf16[2048,300]{0,1:T(8,128)(2,1)}) fusion(f32[2048,300]{0,1:T(8,128)S(1)} %copy-done.3, f32[2048,300]{0,1:T(8,128)} %fusion.17, bf16[4096,2048]{1,0:T(8,128)(2,1)} %param.4, f32[4096,300]{0,1:T(8,128)} %copy-done.2, f32[4096,300]{0,1:T(8,128)} %all-reduce.10.cloned.1.call-done, f32[2048]{0:T(1024)S(1)} %copy-done.4), kind=kOutput, calls=%fused_computation.44 | convolution fusion | flops 5042380800 | bytes 35217408 | tf_op jit(solution)/shard_map/dot_general | solution.py:19
  316.1 18.9 %convolution_bitcast_fusion.4 = f32[4096,300]{0,1:T(8,128)} fusion(bf16[4096,2048]{1,0:T(8,128)(2,1)} %param.4, bf16[2048,300]{0,1:T(8,128)(2,1)} %get-tuple-element.3), kind=kOutput, calls=%fused_computation.4 | convolution fusion | flops 5033164800 | bytes 22921216 | tf_op jit(solution)/shard_map/dot_general | solution.py:22
  335.1 0.3 all-reduce.14.cloned.1.call-start
  335.4 117.3 %all-reduce.12.cloned.1.call-done = f32[4096,300]{0,1:T(8,128)} async-done(((f32[4096,300]{0,1:T(8,128)}), f32[4096,300]{0,1:T(8,128)}) %all-reduce.12.cloned.1.call-update) | async-done | bytes 4915216 | tf_op jit(solution)/shard_map/psum | solution.py:23
  452.7 6.9 multiply_subtract_fusion.4
  459.7 2.3 copy-done
  461.9 10.7 fusion.13
  472.7 19.1 %convolution_bitcast_fusion.3 = f32[4096,300]{0,1:T(8,128)} fusion(bf16[4096,2048]{1,0:T(8,128)(2,1)} %param.4, f32[2048,300]{0,1:T(8,128)} %fusion.13), kind=kOutput, calls=%fused_computation.3 | convolution fusion | flops 5033779200 | bytes 24150016 | tf_op jit(solution)/shard_map/dot_general | solution.py:22
  491.8 0.5 all-reduce.16.cloned.1.call-start
  492.4 117.1 %all-reduce.14.cloned.1.call-done = f32[4096,300]{0,1:T(8,128)} async-done(((f32[4096,300]{0,1:T(8,128)}), f32[4096,300]{0,1:T(8,128)}) %all-reduce.14.cloned.1.call-update) | async-done | bytes 4915216 | tf_op jit(solution)/shard_map/psum | solution.py:23
  609.4 14.0 %multiply_add_fusion.2 = (f32[2048,300]{0,1:T(8,128)S(1)}, bf16[2048,300]{0,1:T(8,128)(2,1)}) fusion(f32[2048,300]{0,1:T(8,128)} %get-tuple-element.2, f32[2048,300]{0,1:T(8,128)} %fusion.13, bf16[4096,2048]{1,0:T(8,128)(2,1)} %param.4, f32[4096,300]{0,1:T(8,128)} %copy-done, f32[4096,300]{0,1:T(8,128)} %all-reduce.14.cloned.1.call-done, f32[2048]{0:T(1024)S(1)} %copy-done.4), kind=kOutput, calls=%fused_computation.40 | convolution fusion | flops 5042380800 | bytes 35217408 | tf_op jit(solution)/shard_map/dot_general | solution.py:19
  623.4 18.9 %convolution_bitcast_fusion.2 = f32[4096,300]{0,1:T(8,128)} fusion(bf16[4096,2048]{1,0:T(8,128)(2,1)} %param.4, bf16[2048,300]{0,1:T(8,128)(2,1)} %get-tuple-element.5), kind=kOutput, calls=%fused_computation.2 | convolution fusion | flops 5033164800 | bytes 22921216 | tf_op jit(solution)/shard_map/dot_general | solution.py:22
  642.4 0.2 all-reduce.18.cloned.1.call-start
  642.6 117.3 %all-reduce.16.cloned.1.call-done = f32[4096,300]{0,1:T(8,128)} async-done(((f32[4096,300]{0,1:T(8,128)}), f32[4096,300]{0,1:T(8,128)}) %all-reduce.16.cloned.1.call-update) | async-done | bytes 4915216 | tf_op jit(solution)/shard_map/psum | solution.py:23
  760.0 6.9 multiply_subtract_fusion.2
  766.9 2.3 copy-done.1
  769.2 10.8 fusion.9
  780.0 19.1 %convolution_bitcast_fusion.1 = f32[4096,300]{0,1:T(8,128)} fusion(bf16[4096,2048]{1,0:T(8,128)(2,1)} %param.4, f32[2048,300]{0,1:T(8,128)} %fusion.9), kind=kOutput, calls=%fused_computation.1 | convolution fusion | flops 5033779200 | bytes 24150016 | tf_op jit(solution)/shard_map/dot_general | solution.py:22
  799.1 0.3 all-reduce.20.cloned.1.call-start
  799.4 117.4 %all-reduce.18.cloned.1.call-done = f32[4096,300]{0,1:T(8,128)} async-done(((f32[4096,300]{0,1:T(8,128)}), f32[4096,300]{0,1:T(8,128)}) %all-reduce.18.cloned.1.call-update) | async-done | bytes 4915216 | tf_op jit(solution)/shard_map/psum | solution.py:23
  916.8 13.7 %multiply_add_fusion = (f32[2048,300]{0,1:T(8,128)}, bf16[2048,300]{0,1:T(8,128)(2,1)}) fusion(f32[2048,300]{0,1:T(8,128)S(1)} %get-tuple-element.4, f32[2048,300]{0,1:T(8,128)} %fusion.9, bf16[4096,2048]{1,0:T(8,128)(2,1)} %param.4, f32[4096,300]{0,1:T(8,128)} %copy-done.1, f32[4096,300]{0,1:T(8,128)} %all-reduce.18.cloned.1.call-done, f32[2048]{0:T(1024)S(1)} %copy-done.4), kind=kOutput, calls=%fused_computation.36 | convolution fusion | flops 5042380800 | bytes 35217408 | tf_op jit(solution)/shard_map/dot_general | solution.py:19
  930.5 18.9 %convolution_bitcast_fusion = f32[4096,300]{0,1:T(8,128)} fusion(bf16[4096,2048]{1,0:T(8,128)(2,1)} %param.4, bf16[2048,300]{0,1:T(8,128)(2,1)} %get-tuple-element.7), kind=kOutput, calls=%fused_computation | convolution fusion | flops 5033164800 | bytes 22921216 | tf_op jit(solution)/shard_map/dot_general | solution.py:22
  949.4 117.7 %all-reduce.20.cloned.1.call-done = f32[4096,300]{0,1:T(8,128)} async-done(((f32[4096,300]{0,1:T(8,128)}), f32[4096,300]{0,1:T(8,128)}) %all-reduce.20.cloned.1.call-update) | async-done | bytes 4915216 | tf_op jit(solution)/shard_map/psum | solution.py:23
  1067.1 9.5 multiply_subtract_fusion
  (18 shorter events, 0.5 us)
Async XLA Ops:
  7.2 140.7 %all-reduce.8.cloned.1.call-start = ((), (), s32[]{:S(2)}) async-start(), calls=%async_computation | async-start | bytes 9961472 | tf_op jit(solution)/shard_map/psum | solution.py:17
  26.3 128.5 %copy-start.3 = (f32[2048,300]{0,1:T(8,128)S(1)}, f32[2048,300]{0,1:T(8,128)}, u32[]{:S(2)}) copy-start(f32[2048,300]{0,1:T(8,128)} %param.6) | copy-start | bytes 7372804
  26.3 128.5 %copy-start.4 = (f32[2048]{0:T(1024)S(1)}, f32[2048]{0:T(1024)}, u32[]{:S(2)}) copy-start(f32[2048]{0:T(1024)} %param.7) | copy-start | bytes 24580
  26.3 276.1 %all-reduce.10.cloned.1.call-start = ((), (), s32[]{:S(2)}) async-start(), calls=%async_computation.1 | async-start | bytes 9961472 | tf_op jit(solution)/shard_map/psum | solution.py:23
  152.6 2.3 copy-start.2
  184.8 268.0 %all-reduce.12.cloned.1.call-start = ((), (), s32[]{:S(2)}) async-start(), calls=%async_computation.2 | async-start | bytes 9961472 | tf_op jit(solution)/shard_map/psum | solution.py:23
  335.1 126.9 %copy-start.5 = (f32[2048,300]{0,1:T(8,128)S(1)}, f32[2048,300]{0,1:T(8,128)}, u32[]{:S(2)}) copy-start(f32[2048,300]{0,1:T(8,128)} %get-tuple-element.2) | copy-start | bytes 7372804
  335.1 274.4 %all-reduce.14.cloned.1.call-start = ((), (), s32[]{:S(2)}) async-start(), calls=%async_computation.3 | async-start | bytes 9961472 | tf_op jit(solution)/shard_map/psum | solution.py:23
  459.7 2.3 copy-start
  491.8 268.1 %all-reduce.16.cloned.1.call-start = ((), (), s32[]{:S(2)}) async-start(), calls=%async_computation.4 | async-start | bytes 9961472 | tf_op jit(solution)/shard_map/psum | solution.py:23
  642.4 274.4 %all-reduce.18.cloned.1.call-start = ((), (), s32[]{:S(2)}) async-start(), calls=%async_computation.5 | async-start | bytes 9961472 | tf_op jit(solution)/shard_map/psum | solution.py:23
  766.9 2.3 copy-start.1
  799.1 268.0 %all-reduce.20.cloned.1.call-start = ((), (), s32[]{:S(2)}) async-start(), calls=%async_computation.6 | async-start | bytes 9961472 | tf_op jit(solution)/shard_map/psum | solution.py:23
Sparse Core Ops, SparseCore 0:
  26.4 121.3 all-reduce.7
  184.9 117.5 all-reduce.9
  335.2 117.5 all-reduce.11
  492.0 117.4 all-reduce.13
  642.5 117.4 all-reduce.15
  799.2 117.5 all-reduce.17
  949.5 117.4 all-reduce.19
where the time goes:
time: 1090 us; the launch traced here: 1080 us
  waiting for transfers between devices  826 us (76%)
  matrix products  207 us (19%)
  other arithmetic  28.1 us (3%)
  between operations  14.5 us (1%)
    psum x6, waiting for transfers between devices, local_solve(): residual = residual - MIX_WEIGHT * lax.psum(contrib, 'feat')  704 us
    psum x1, waiting for transfers between devices, local_solve(): residual = targets - lax.psum(partial, 'feat')  121 us
    dot_general x6, matrix products, local_solve(): jnp.dot(design, update.astype(jnp.bfloat16), preferred_element_type=jnp.f...  114 us
    dot_general x6, matrix products, local_solve(): lax.dot_general(design, residual.astype(jnp.bfloat16), (((0,), (0,)), (()...  73.6 us
    sub x3, other arithmetic, local_solve(): residual = residual - MIX_WEIGHT * lax.psum(contrib, 'feat')  23.4 us
  transfers between devices with their start and end apart: 7, of which 7 were waited for; matrix products, arithmetic and copies ran while one was open for 0% of the time, Pallas kernels for 0%

commit v1 on v0

v1 whole, which is shorter than its diff:
```python
import functools

import jax
import jax.numpy as jnp
from jax import lax
from jax.experimental import pallas as pl
from jax.experimental.pallas import tpu as pltpu
from jax.sharding import PartitionSpec as P

SWEEPS = 6
RIDGE_COEF = 1.0
MIX_WEIGHT = 0.75
CORES = 2
ROW_TILE = 16
MESH = pl.DeviceIdType.MESH


def split_rows(padded):
    first = -(-padded // (2 * ROW_TILE)) * ROW_TILE
    return ((0, first), (first, padded - first))


def kernel(chips, samples, streams, x_hbm, w_hbm, y_hbm, eta_ref, wout_hbm, rout_hbm,
           x, w, res, grad, op, xsem, wsem, ysem, wosem, *rest):
    per = len(rest) // len(streams)
    st = [rest[i * per:(i + 1) * per] for i in range(len(streams))]
    far, near = chips // 2, chips - 1 - chips // 2
    block = samples // (chips * CORES)
    rows_chip = block * CORES
    depth = x.shape[1]
    ridge_val = RIDGE_COEF / samples

    prob = lax.axis_index("prob")
    feat = lax.axis_index("feat")
    z, c = feat // CORES, feat % CORES
    other = 1 - c
    sgn = 1 - 2 * c

    def chip_at(v):
        return lax.rem(z + v * sgn + chips, chips)

    sib = (prob, z * CORES + other)
    nbr_p = (prob, chip_at(1) * CORES + c)
    nbr_q = (prob, chip_at(-1) * CORES + c)

    def x_rows(v):
        return pl.ds(pl.multiple_of(chip_at(v) * rows_chip, rows_chip), rows_chip)

    def remote(src, dst, ssem, rsem, dev):
        return pltpu.make_async_remote_copy(src_ref=src, dst_ref=dst, send_sem=ssem, recv_sem=rsem,
                                            device_id=dev, device_id_type=MESH)

    def x_copy(v):
        return pltpu.make_async_copy(x_hbm.at[x_rows(v), :], x.at[x_rows(v), :], xsem.at[v % chips])

    class Stream:
        def __init__(self, index):
            self.r0, self.rows = streams[index]
            self.rs = pl.ds(self.r0, self.rows)
            (self.pbuf, self.precv, self.rp, self.rq, self.rbf, self.rfin,
             self.pd_s, self.pd_r, self.rsp_s, self.rsp_r, self.rsq_s, self.rsq_r,
             self.agp_s, self.agp_r, self.agq_s, self.agq_r, self.agd_s, self.agd_r, self.osem) = st[index]

        def pd(self, v):
            a, b = v % chips, -v % chips
            return remote(self.pbuf.at[a, other], self.precv.at[b], self.pd_s.at[a], self.pd_r.at[b], sib)

        def rs_p(self, t):
            return remote(self.pbuf.at[far + 1 - t, c], self.rp.at[t - 1], self.rsp_s.at[t - 1],
                          self.rsp_r.at[t - 1], nbr_p)

        def rs_q(self, t):
            return remote(self.pbuf.at[-(near + 1 - t) % chips, c], self.rq.at[t - 1], self.rsq_s.at[t - 1],
                          self.rsq_r.at[t - 1], nbr_q)

        def ag_p(self, buf, t):
            return remote(buf.at[t - 1, c], buf.at[t, c], self.agp_s.at[t - 1], self.agp_r.at[t - 1], nbr_p)

        def ag_q(self, buf, t):
            return remote(buf.at[-(t - 1) % chips, c], buf.at[-t % chips, c], self.agq_s.at[t - 1],
                          self.agq_r.at[t - 1], nbr_q)

        def ag_d(self, buf, u):
            a, b = u % chips, -u % chips
            return remote(buf.at[a, c], buf.at[b, c], self.agd_s.at[a], self.agd_r.at[b], sib)

        def ag_d_in(self, buf, u):
            a = u % chips
            return remote(buf.at[a, other], buf.at[a, other], self.agd_s.at[a], self.agd_r.at[a], sib)

        def product(self, v):
            out = lax.dot_general(op[self.rs, :], x[x_rows(v), :], (((1,), (1,)), ((), ())),
                                  preferred_element_type=jnp.float32)
            for core in range(CORES):
                self.pbuf[v % chips, core] = out[:, core * block:(core + 1) * block]
            self.pd(v).start()

        def pass_on(self, t):
            v = far + 1 - t
            self.pd(-v).wait_recv()
            total = self.pbuf[v, c] + self.precv[v]
            if t > 1:
                self.rs_p(t - 1).wait_recv()
                total = total + self.rp[t - 2]
            self.pbuf[v, c] = total
            self.rs_p(t).start()
            t = t - 1
            if t >= 1:
                v = near + 1 - t
                slot = -v % chips
                self.pd(v).wait_recv()
                total = self.pbuf[slot, c] + self.precv[slot]
                if t > 1:
                    self.rs_q(t - 1).wait_recv()
                    total = total + self.rq[t - 2]
                self.pbuf[slot, c] = total
                self.rs_q(t).start()

        def finish(self, it):
            self.pd(0).wait_recv()
            total = self.pbuf[0, c] + self.precv[0]
            self.rs_p(far).wait_recv()
            self.rs_q(near).wait_recv()
            total = total + self.rp[far - 1] + self.rq[near - 1]
            coef = jnp.where(it == 0, 1.0, MIX_WEIGHT).astype(jnp.float32)
            new = res[self.rs, :] - coef * total
            res[self.rs, :] = new

            @pl.when(it < SWEEPS)
            def _():
                self.rbf[0, c] = new.astype(jnp.bfloat16)
                self.ag_open(self.rbf)

            @pl.when(it == SWEEPS)
            def _():
                self.rfin[0, c] = new
                self.ag_open(self.rfin)

        def ag_open(self, buf):
            self.ag_p(buf, 1).start()
            self.ag_q(buf, 1).start()
            self.ag_d(buf, 0).start()

        def ag_step(self, buf, t):
            self.ag_p(buf, t).wait_recv()
            if t < far:
                self.ag_p(buf, t + 1).start()
            if t <= near:
                self.ag_q(buf, t).wait_recv()
                if t < near:
                    self.ag_q(buf, t + 1).start()
            self.ag_d(buf, t).start()
            if t <= near:
                self.ag_d(buf, -t).start()

        def settle_sums(self):
            for v in range(chips):
                self.pd(v).wait_send()
            for t in range(1, far + 1):
                self.rs_p(t).wait_send()
            for t in range(1, near + 1):
                self.rs_q(t).wait_send()

        def settle_gather(self, buf):
            for t in range(1, far + 1):
                self.ag_p(buf, t).wait_send()
            for t in range(1, near + 1):
                self.ag_q(buf, t).wait_send()
            for u in range(chips):
                self.ag_d(buf, u).wait_send()

        def gradient(self, t):
            offsets = (t, -t) if 0 < t <= near else (t,)
            parts = []
            for u in offsets:
                self.ag_d_in(self.rbf, u).wait_recv()
                parts.append((jnp.concatenate([self.rbf[u % chips, core] for core in range(CORES)], axis=1), x_rows(-u)))
            wide = min(depth, 1024)
            for j in range(depth // wide):
                cols = pl.ds(j * wide, wide)
                total = None if t == 0 else grad[self.rs, cols]
                for lhs, where in parts:
                    term = jnp.dot(lhs, x[where, cols], preferred_element_type=jnp.float32)
                    total = term if total is None else total + term
                grad[self.rs, cols] = total

        def step(self):
            @pl.loop(0, self.rows // ROW_TILE)
            def _(i):
                rs = pl.ds(pl.multiple_of(self.r0 + i * ROW_TILE, ROW_TILE), ROW_TILE)
                old = w[rs, :]
                update = eta_ref[...] * (grad[rs, :] * (1.0 / samples) - ridge_val * old)
                w[rs, :] = old + MIX_WEIGHT * update
                op[rs, :] = update.astype(jnp.bfloat16)

        def cast(self):
            @pl.loop(0, self.rows // ROW_TILE)
            def _(i):
                rs = pl.ds(pl.multiple_of(self.r0 + i * ROW_TILE, ROW_TILE), ROW_TILE)
                op[rs, :] = w[rs, :].astype(jnp.bfloat16)

        def write(self, u, core):
            return pltpu.make_async_copy(self.rfin.at[u % chips, core],
                                         rout_hbm.at[chip_at(-u) * CORES + core, self.rs, :],
                                         self.osem.at[u % chips, core])

    group = [Stream(i) for i in range(len(streams))]
    order = [far] + [s * v for v in range(near, 0, -1) for s in (1, -1)] + [0]

    w_copy = pltpu.make_async_copy(w_hbm, w, wsem)
    w_copy.start()
    x_copy(far).start()
    for v in order[1:]:
        x_copy(v).start()
    y_copy = pltpu.make_async_copy(y_hbm, res, ysem)
    y_copy.start()

    barrier = pltpu.get_barrier_semaphore()
    for dev in (sib, nbr_p, nbr_q):
        pl.semaphore_signal(barrier, inc=1, device_id=dev, device_id_type=MESH)
    pl.semaphore_wait(barrier, 3)

    w_copy.wait()
    for s in group:
        s.cast()
    x_copy(far).wait()
    for s in group:
        s.product(far)
    y_copy.wait()

    @pl.loop(0, SWEEPS + 1)
    def _(it):
        def products(s, vs):
            for v in vs:
                if s is group[0]:
                    @pl.when(it == 0)
                    def _():
                        x_copy(v).wait()
                s.product(v)

        for t in range(1, far + 1):
            v = far - t
            vs = (v, -v) if v else (0,)
            for s in group:
                s.pass_on(t)
                products(s, vs)
        for s in group:
            s.finish(it)
        for s in group:
            s.settle_sums()

        @pl.when(it < SWEEPS)
        def _():
            for t in range(1, far + 1):
                for s in group:
                    s.ag_step(s.rbf, t)
                    s.gradient(t - 1)
            for s in group:
                s.gradient(far)
                s.step()
                s.settle_gather(s.rbf)
                s.product(far)

    w_out = pltpu.make_async_copy(w, wout_hbm, wosem)
    w_out.start()
    for s in group:
        s.write(0, c).start()
    for t in range(1, far + 1):
        for s in group:
            s.ag_step(s.rfin, t)
            s.write(t, c).start()
            if t <= near:
                s.write(-t, c).start()
            us = (0,) if t == 1 else (t - 1, 1 - t)
            for u in us:
                s.ag_d_in(s.rfin, u).wait_recv()
                s.write(u, other).start()
    for s in group:
        s.ag_d_in(s.rfin, far).wait_recv()
        s.write(far, other).start()
    for s in group:
        s.settle_gather(s.rfin)
        for u in range(chips):
            for core in (c, other):
                s.write(u, core).wait()
    w_out.wait()


def solve(chips, design, w_t, y_t, eta):
    samples, depth = design.shape
    padded = w_t.shape[0]
    block = y_t.shape[1]
    far, near = chips // 2, chips - 1 - chips // 2
    streams = split_rows(padded)
    dma = pltpu.SemaphoreType.DMA
    f32, bf16 = jnp.float32, jnp.bfloat16
    scratch = [
        pltpu.VMEM((samples, depth), bf16),
        pltpu.VMEM((padded, depth), f32),
        pltpu.VMEM((padded, block), f32),
        pltpu.VMEM((padded, depth), f32),
        pltpu.VMEM((padded, depth), bf16),
        dma((chips,)), dma, dma, dma,
    ]
    for _, rows in streams:
        scratch += [
            pltpu.VMEM((chips, CORES, rows, block), f32),
            pltpu.VMEM((chips, rows, block), f32),
            pltpu.VMEM((far, rows, block), f32),
            pltpu.VMEM((near, rows, block), f32),
            pltpu.VMEM((chips, CORES, rows, block), bf16),
            pltpu.VMEM((chips, CORES, rows, block), f32),
            dma((chips,)), dma((chips,)),
            dma((far,)), dma((far,)), dma((near,)), dma((near,)),
            dma((far,)), dma((far,)), dma((near,)), dma((near,)),
            dma((chips,)), dma((chips,)),
            dma((chips, CORES)),
        ]
    any_spec = pl.BlockSpec(memory_space=pl.ANY)
    return pl.pallas_call(
        functools.partial(kernel, chips, samples, streams),
        out_shape=(jax.ShapeDtypeStruct((padded, depth), f32),
                   jax.ShapeDtypeStruct((chips * CORES, padded, block), f32)),
        in_specs=[any_spec, any_spec, any_spec, pl.BlockSpec(memory_space=pltpu.VMEM)],
        out_specs=(any_spec, any_spec),
        scratch_shapes=scratch,
        compiler_params=pltpu.CompilerParams(collective_id=0, has_side_effects=True,
                                             vmem_limit_bytes=56 * 1024 * 1024),
    )(design, w_t, y_t, eta)


def solution(mesh):
    feats = mesh.shape["feat"]

    def local_solve(design, targets, weights, step_sizes):
        samples, depth = design.shape
        k = targets.shape[1]
        padded = -(-k // ROW_TILE) * ROW_TILE
        block = samples // feats
        pad = ((0, padded - k), (0, 0))
        w_t = jnp.pad(weights.T, pad)
        mine = lax.dynamic_slice_in_dim(targets, lax.axis_index("feat") * block, block, 0)
        y_t = jnp.pad(mine.T, pad)
        w_new, r_new = solve(feats // CORES, design, w_t, y_t, step_sizes[None, :])
        residual = r_new[:, :k, :].transpose(0, 2, 1).reshape(samples, k)
        return w_new[:k].T, residual

    return jax.shard_map(
        local_solve,
        mesh=mesh,
        in_specs=(P('prob', 'feat'), P('prob', None), P(('prob', 'feat'), None), P(('prob', 'feat'))),
        out_specs=(P(('prob', 'feat'), None), P('prob', None)),
        check_vma=False,
    )
```

time: 1090 us -> 365 us (0.33)
  waiting for transfers between devices: 826 us -> 0 us
  Pallas kernels: 0 us -> 344 us
  matrix products: 207 us -> 0 us
  other arithmetic: 28.1 us -> 0 us
  between operations: 14.5 us -> 0.68 us
  local copies, waits for them, and re-layouts: 6.82 us -> 19.4 us
    psum x7 -> x0, waiting for transfers between devices: 826 us -> none  [the longest x6 704 us: local_solve(): residual = residual - MIX_WEIGHT * lax.psum(contrib, 'feat')]
    pallas_call x0 -> x1, Pallas kernels: none -> 344 us  [solve(): pl.pallas_call(functools.partial(kernel, chips, samples, streams), out_sh...]
    dot_general x13 -> x0, matrix products: 207 us -> none  [the longest x6 114 us: local_solve(): jnp.dot(design, update.astype(jnp.bfloat16), preferred_element_type=jnp.f...]
    sub x4 -> x0, other arithmetic: 28.1 us -> none  [the longest x3 23.4 us: local_solve(): residual = residual - MIX_WEIGHT * lax.psum(contrib, 'feat')]
  transfers between devices with their start and end apart: 7 -> 0, of which waited for: 7 -> 0; matrix products, arithmetic and copies ran while one was open for 0% -> 0% of each run, Pallas kernels for 0% -> 0%
where the time goes in v1:
time: 365 us; the launch traced here: 364 us
  Pallas kernels  344 us (94%)
  local copies, waits for them, and re-layouts  19.4 us (5%)
    pallas_call x1, Pallas kernels, solve(): pl.pallas_call(functools.partial(kernel, chips, samples, streams), out_sh...  344 us
    unnamed x4, local copies, waits for them, and re-layouts  7.41 us

profile of v1, /device:TPU:21, one launch (start us, length us, event | category | flops | bytes accessed | tf_op | source)
XLA Modules:
  0.0 364.4 jit_solution(6071470322020449709)
XLA Ops:
  0.6 1.0 dynamic-slice_bitcast_fusion
  1.6 0.7 pad.9.y_hbm
  2.4 3.4 pad.8.w_hbm
  5.8 344.3 %shard_map.59 = (f32[304,2048]{1,0:T(8,128)}, f32[16,304,256]{2,1,0:T(8,128)}) custom-call(bf16[4096,2048]{1,0:T(8,128)(2,1)} %x_hbm.1, f32[304,2048]{1,0:T(8,128)} %pad.8.w_hbm, f32[304,256]{1,0:T(8,128)} %pad.9.y_hbm, f32[1,2048]{1,0:T(1,128)} %bitcast.19), custom_call_target="tpu_custom_call" | custom-call | tf_op jit(solution)/shard_map/pallas_call | solution.py:320
  350.1 0.0 copy-start
  350.2 3.6 slice_bitcast_fusion.1
  353.7 0.0 copy-done
  353.7 0.4 slice_bitcast_fusion
  354.1 2.8 copy.9
  357.0 0.5 pad.10
  357.5 6.9 %copy.7 = f32[38,8,16,256]{3,1,2,0:T(8,128)} copy(f32[38,8,16,256]{3,2,1,0:T(8,128)S(1)} %bitcast.15) | data formatting | bytes 9961472
Async XLA Ops:
  350.1 3.6 copy-start

commit v2 on v1

v2 whole, which is shorter than its diff:
```python
import functools

import jax
import jax.numpy as jnp
from jax import lax
from jax.experimental import pallas as pl
from jax.experimental.pallas import tpu as pltpu
from jax.sharding import PartitionSpec as P

SWEEPS = 6
RIDGE_COEF = 1.0
MIX_WEIGHT = 0.75
CORES = 2
ROW_TILE = 16
PIECES = 2
MESH = pl.DeviceIdType.MESH


def split_rows(padded):
    first = -(-padded // (2 * ROW_TILE)) * ROW_TILE
    return ((0, first), (first, padded - first))


def split_pieces(rows):
    size = -(-rows // (PIECES * ROW_TILE)) * ROW_TILE
    return tuple((r, min(size, rows - r)) for r in range(0, rows, size))


def kernel(chips, samples, streams, x_hbm, w_hbm, y_hbm, eta_ref, wout_hbm, rout_hbm,
           x, wraw, yraw, w, res, grad, op, xsem, wsem, ysem, wosem, *rest):
    per = len(rest) // len(streams)
    st = [rest[i * per:(i + 1) * per] for i in range(len(streams))]
    far, near = chips // 2, chips - 1 - chips // 2
    block = samples // (chips * CORES)
    rows_chip = block * CORES
    depth = x.shape[1]
    ridge_val = RIDGE_COEF / samples

    prob = lax.axis_index("prob")
    feat = lax.axis_index("feat")
    z, c = feat // CORES, feat % CORES
    other = 1 - c
    sgn = 1 - 2 * c

    def chip_at(v):
        return lax.rem(z + v * sgn + chips, chips)

    sib = (prob, z * CORES + other)
    nbr_p = (prob, chip_at(1) * CORES + c)
    nbr_q = (prob, chip_at(-1) * CORES + c)

    def x_rows(v):
        return pl.ds(pl.multiple_of(chip_at(v) * rows_chip, rows_chip), rows_chip)

    def remote(src, dst, ssem, rsem, dev):
        return pltpu.make_async_remote_copy(src_ref=src, dst_ref=dst, send_sem=ssem, recv_sem=rsem,
                                            device_id=dev, device_id_type=MESH)

    def x_copy(v):
        return pltpu.make_async_copy(x_hbm.at[x_rows(v), :], x.at[x_rows(v), :], xsem.at[v % chips])

    class Stream:
        def __init__(self, index):
            self.r0, self.rows = streams[index]
            self.rs = pl.ds(self.r0, self.rows)
            self.cuts = split_pieces(self.rows)
            self.pieces = range(len(self.cuts))
            (self.pbuf, self.precv, self.rp, self.rq, self.rbf, self.rfin,
             self.pd_s, self.pd_r, self.rsp_s, self.rsp_r, self.rsq_s, self.rsq_r,
             self.agp_s, self.agp_r, self.agq_s, self.agq_r, self.agd_s, self.agd_r, self.osem) = st[index]

        def ps(self, p):
            return pl.ds(*self.cuts[p])

        def pd(self, v):
            a, b = v % chips, -v % chips
            return remote(self.pbuf.at[a, other], self.precv.at[b], self.pd_s.at[a], self.pd_r.at[b], sib)

        def rs_p(self, t, p):
            ps = self.ps(p)
            return remote(self.pbuf.at[far + 1 - t, c, ps], self.rp.at[t - 1, ps], self.rsp_s.at[t - 1, p],
                          self.rsp_r.at[t - 1, p], nbr_p)

        def rs_q(self, t, p):
            ps = self.ps(p)
            return remote(self.pbuf.at[-(near + 1 - t) % chips, c, ps], self.rq.at[t - 1, ps],
                          self.rsq_s.at[t - 1, p], self.rsq_r.at[t - 1, p], nbr_q)

        def ag_p(self, buf, t, p):
            ps = self.ps(p)
            return remote(buf.at[t - 1, c, ps], buf.at[t, c, ps], self.agp_s.at[t - 1, p],
                          self.agp_r.at[t - 1, p], nbr_p)

        def ag_q(self, buf, t, p):
            ps = self.ps(p)
            return remote(buf.at[-(t - 1) % chips, c, ps], buf.at[-t % chips, c, ps], self.agq_s.at[t - 1, p],
                          self.agq_r.at[t - 1, p], nbr_q)

        def ag_d(self, buf, u, p):
            a, b, ps = u % chips, -u % chips, self.ps(p)
            return remote(buf.at[a, c, ps], buf.at[b, c, ps], self.agd_s.at[a, p], self.agd_r.at[b, p], sib)

        def ag_d_in(self, buf, u, p):
            a, ps = u % chips, self.ps(p)
            return remote(buf.at[a, other, ps], buf.at[a, other, ps], self.agd_s.at[a, p], self.agd_r.at[a, p], sib)

        def product(self, v):
            out = lax.dot_general(op[self.rs, :], x[x_rows(v), :], (((1,), (1,)), ((), ())),
                                  preferred_element_type=jnp.float32)
            for core in range(CORES):
                self.pbuf[v % chips, core] = out[:, core * block:(core + 1) * block]
            self.pd(v).start()

        def pass_on(self, t, p):
            ps = self.ps(p)
            v = far + 1 - t
            if p == 0:
                self.pd(-v).wait_recv()
            total = self.pbuf[v, c, ps] + self.precv[v, ps]
            if t > 1:
                self.rs_p(t - 1, p).wait_recv()
                total = total + self.rp[t - 2, ps]
            self.pbuf[v, c, ps] = total
            self.rs_p(t, p).start()
            t = t - 1
            if t >= 1:
                v = near + 1 - t
                slot = -v % chips
                if p == 0:
                    self.pd(v).wait_recv()
                total = self.pbuf[slot, c, ps] + self.precv[slot, ps]
                if t > 1:
                    self.rs_q(t - 1, p).wait_recv()
                    total = total + self.rq[t - 2, ps]
                self.pbuf[slot, c, ps] = total
                self.rs_q(t, p).start()

        def finish(self, it, p):
            ps = self.ps(p)
            if p == 0:
                self.pd(0).wait_recv()
            total = self.pbuf[0, c, ps] + self.precv[0, ps]
            self.rs_p(far, p).wait_recv()
            self.rs_q(near, p).wait_recv()
            total = total + self.rp[far - 1, ps] + self.rq[near - 1, ps]
            coef = jnp.where(it == 0, 1.0, MIX_WEIGHT).astype(jnp.float32)
            start, size = self.cuts[p]
            rs = pl.ds(self.r0 + start, size)
            new = res[rs, :] - coef * total
            res[rs, :] = new

            @pl.when(it < SWEEPS)
            def _():
                self.rbf[0, c, ps] = new.astype(jnp.bfloat16)
                self.ag_open(self.rbf, p)

            @pl.when(it == SWEEPS)
            def _():
                self.rfin[0, c, ps] = new
                self.ag_open(self.rfin, p)

        def ag_open(self, buf, p):
            self.ag_p(buf, 1, p).start()
            self.ag_q(buf, 1, p).start()
            self.ag_d(buf, 0, p).start()

        def ag_step(self, buf, t, p):
            self.ag_p(buf, t, p).wait_recv()
            if t < far:
                self.ag_p(buf, t + 1, p).start()
            self.ag_d(buf, t, p).start()
            if t <= near:
                self.ag_q(buf, t, p).wait_recv()
                if t < near:
                    self.ag_q(buf, t + 1, p).start()
                self.ag_d(buf, -t, p).start()

        def settle_sums(self):
            for v in range(chips):
                self.pd(v).wait_send()
            for p in self.pieces:
                for t in range(1, far + 1):
                    self.rs_p(t, p).wait_send()
                for t in range(1, near + 1):
                    self.rs_q(t, p).wait_send()

        def settle_gather(self, buf):
            for p in self.pieces:
                for t in range(1, far + 1):
                    self.ag_p(buf, t, p).wait_send()
                for t in range(1, near + 1):
                    self.ag_q(buf, t, p).wait_send()
                for u in range(chips):
                    self.ag_d(buf, u, p).wait_send()

        def gradient(self, t):
            offsets = (t, -t) if 0 < t <= near else (t,)
            parts = []
            for u in offsets:
                for p in self.pieces:
                    self.ag_d_in(self.rbf, u, p).wait_recv()
                parts.append((jnp.concatenate([self.rbf[u % chips, core] for core in range(CORES)], axis=1), x_rows(-u)))
            wide = min(depth, 1024)
            for j in range(depth // wide):
                cols = pl.ds(j * wide, wide)
                total = None if t == 0 else grad[self.rs, cols]
                for lhs, where in parts:
                    term = jnp.dot(lhs, x[where, cols], preferred_element_type=jnp.float32)
                    total = term if total is None else total + term
                grad[self.rs, cols] = total

        def step(self):
            @pl.loop(0, self.rows // ROW_TILE)
            def _(i):
                rs = pl.ds(pl.multiple_of(self.r0 + i * ROW_TILE, ROW_TILE), ROW_TILE)
                old = w[rs, :]
                update = eta_ref[...] * (grad[rs, :] * (1.0 / samples) - ridge_val * old)
                w[rs, :] = old + MIX_WEIGHT * update
                op[rs, :] = update.astype(jnp.bfloat16)

        def cast(self):
            k = wraw.shape[0]
            real = min(self.rows, k - self.r0)

            def move(rs):
                rows = wraw[rs, :]
                w[rs, :] = rows
                op[rs, :] = rows.astype(jnp.bfloat16)

            @pl.loop(0, real // ROW_TILE)
            def _(i):
                move(pl.ds(pl.multiple_of(self.r0 + i * ROW_TILE, ROW_TILE), ROW_TILE))

            if real % ROW_TILE:
                move(pl.ds(self.r0 + real // ROW_TILE * ROW_TILE, real % ROW_TILE))

        def write(self, u, core):
            return pltpu.make_async_copy(self.rfin.at[u % chips, core],
                                         rout_hbm.at[self.rs, pl.ds(pl.multiple_of((chip_at(-u) * CORES + core) * block, block), block)],
                                         self.osem.at[u % chips, core])

    group = [Stream(i) for i in range(len(streams))]
    order = [far] + [s * v for v in range(near, 0, -1) for s in (1, -1)] + [0]

    w_copy = pltpu.make_async_copy(w_hbm, wraw, wsem)
    w_copy.start()
    x_copy(far).start()
    for v in order[1:]:
        x_copy(v).start()
    mine = pl.ds(pl.multiple_of(feat * block, block), block)
    y_copy = pltpu.make_async_copy(y_hbm.at[:, mine], yraw, ysem)
    y_copy.start()

    barrier = pltpu.get_barrier_semaphore()
    for dev in (sib, nbr_p, nbr_q):
        pl.semaphore_signal(barrier, inc=1, device_id=dev, device_id_type=MESH)
    pl.semaphore_wait(barrier, 3)

    w_copy.wait()
    for s in group:
        s.cast()
    x_copy(far).wait()
    for s in group:
        s.product(far)
    y_copy.wait()
    res[pl.ds(0, yraw.shape[0]), :] = yraw[...]

    @pl.loop(0, SWEEPS + 1)
    def _(it):
        def products(s, vs):
            for v in vs:
                if s is group[0]:
                    @pl.when(it == 0)
                    def _():
                        x_copy(v).wait()
                s.product(v)

        for t in range(1, far + 1):
            v = far - t
            vs = (v, -v) if v else (0,)
            for s in group:
                for p in s.pieces:
                    s.pass_on(t, p)
                products(s, vs)
        for s in group:
            for p in s.pieces:
                s.finish(it, p)
        for s in group:
            s.settle_sums()

        @pl.when(it < SWEEPS)
        def _():
            for t in range(1, far + 1):
                for s in group:
                    for p in s.pieces:
                        s.ag_step(s.rbf, t, p)
                    s.gradient(t - 1)
                    if t == far:
                        s.gradient(far)
                        s.step()
                        s.settle_gather(s.rbf)
                        s.product(far)

    w_out = pltpu.make_async_copy(w, wout_hbm, wosem)
    w_out.start()

    def write_in(s, u):
        for p in s.pieces:
            s.ag_d_in(s.rfin, u, p).wait_recv()
        s.write(u, other).start()

    for s in group:
        s.write(0, c).start()
    for t in range(1, far + 1):
        for s in group:
            for p in s.pieces:
                s.ag_step(s.rfin, t, p)
            s.write(t, c).start()
            if t <= near:
                s.write(-t, c).start()
            for u in ((0,) if t == 1 else (t - 1, 1 - t)):
                write_in(s, u)
    for s in group:
        write_in(s, far)
    for s in group:
        s.settle_gather(s.rfin)
        for u in range(chips):
            for core in (c, other):
                s.write(u, core).wait()
    w_out.wait()


def solve(chips, design, w_t, y_t, eta):
    samples, depth = design.shape
    padded = -(-w_t.shape[0] // ROW_TILE) * ROW_TILE
    block = samples // (chips * CORES)
    far, near = chips // 2, chips - 1 - chips // 2
    streams = split_rows(padded)
    dma = pltpu.SemaphoreType.DMA
    f32, bf16 = jnp.float32, jnp.bfloat16
    scratch = [
        pltpu.VMEM((samples, depth), bf16),
        pltpu.VMEM((w_t.shape[0], depth), f32),
        pltpu.VMEM((w_t.shape[0], block), f32),
        pltpu.VMEM((padded, depth), f32),
        pltpu.VMEM((padded, block), f32),
        pltpu.VMEM((padded, depth), f32),
        pltpu.VMEM((padded, depth), bf16),
        dma((chips,)), dma, dma, dma,
    ]
    for _, rows in streams:
        scratch += [
            pltpu.VMEM((chips, CORES, rows, block), f32),
            pltpu.VMEM((chips, rows, block), f32),
            pltpu.VMEM((far, rows, block), f32),
            pltpu.VMEM((near, rows, block), f32),
            pltpu.VMEM((chips, CORES, rows, block), bf16),
            pltpu.VMEM((chips, CORES, rows, block), f32),
            dma((chips,)), dma((chips,)),
            *[dma((hops, PIECES)) for hops in (far, far, near, near) * 2],
            dma((chips, PIECES)), dma((chips, PIECES)),
            dma((chips, CORES)),
        ]
    any_spec = pl.BlockSpec(memory_space=pl.ANY)
    return pl.pallas_call(
        functools.partial(kernel, chips, samples, streams),
        out_shape=(jax.ShapeDtypeStruct((padded, depth), f32),
                   jax.ShapeDtypeStruct((padded, samples), f32)),
        in_specs=[any_spec, any_spec, any_spec, pl.BlockSpec(memory_space=pltpu.VMEM)],
        out_specs=(any_spec, any_spec),
        scratch_shapes=scratch,
        compiler_params=pltpu.CompilerParams(collective_id=0, has_side_effects=True,
                                             vmem_limit_bytes=56 * 1024 * 1024),
    )(design, w_t, y_t, eta)


def trim_kernel(k, w_in, r_in, w_out, r_out):
    w_out[...] = w_in[:k, :]
    r_out[...] = r_in[:k, :]


def trim(k, steps, w_t, r_t):
    def spec(rows, arr):
        return pl.BlockSpec((rows, arr.shape[1] // steps), lambda i: (0, i))

    return pl.pallas_call(
        functools.partial(trim_kernel, k),
        out_shape=tuple(jax.ShapeDtypeStruct((k, a.shape[1]), a.dtype) for a in (w_t, r_t)),
        grid=(steps,),
        in_specs=[spec(a.shape[0], a) for a in (w_t, r_t)],
        out_specs=tuple(spec(k, a) for a in (w_t, r_t)),
    )(w_t, r_t)


def solution(mesh):
    feats = mesh.shape["feat"]

    def local_solve(design, targets, weights, step_sizes):
        w_t, r_t = solve(feats // CORES, design, weights.T, targets.T, step_sizes[None, :])
        w_t, r_t = trim(targets.shape[1], feats // CORES, w_t, r_t)
        return w_t.T, r_t.T

    return jax.shard_map(
        local_solve,
        mesh=mesh,
        in_specs=(P('prob', 'feat'), P('prob', None), P(('prob', 'feat'), None), P(('prob', 'feat'))),
        out_specs=(P(('prob', 'feat'), None), P('prob', None)),
        check_vma=False,
    )
```

time: 365 us -> 344 us (0.942)
  local copies, waits for them, and re-layouts: 19.4 us -> 0 us
    pallas_call x1, Pallas kernels: 344 us -> 334 us  [solve(): pl.pallas_call(functools.partial(kernel, chips, samples, streams), out_sh...]
    pallas_call x0 -> x1, Pallas kernels: none -> 8.39 us  [trim(): pl.pallas_call(functools.partial(trim_kernel, k), out_shape=tuple((jax.Sh...]
    transpose x4 -> x0, local copies, waits for them, and re-layouts: 7.8 us -> none  [the longest x1 3.58 us: local_solve(): return (w_new[:k].T, residual)]
    unnamed x4 -> x0, local copies, waits for them, and re-layouts: 7.41 us -> none
    pad x2 -> x0, local copies, waits for them, and re-layouts: 4.16 us -> none  [the longest x1 3.42 us: local_solve(): w_t = jnp.pad(weights.T, pad)]
where the time goes in v2:
time: 344 us; the launch traced here: 343 us
  Pallas kernels  343 us (100%)
    pallas_call x1, Pallas kernels, solve(): pl.pallas_call(functools.partial(kernel, chips, samples, streams), out_sh...  334 us
    pallas_call x1, Pallas kernels, trim(): pl.pallas_call(functools.partial(trim_kernel, k), out_shape=tuple((jax.Sh...  8.39 us

profile of v2, /device:TPU:21, one launch (start us, length us, event | category | flops | bytes accessed | tf_op | source)
XLA Modules:
  0.0 343.4 jit_solution(12633658334594176239)
XLA Ops:
  0.6 334.3 %shard_map.59 = (f32[304,2048]{1,0:T(8,128)}, f32[304,4096]{1,0:T(8,128)}) custom-call(bf16[4096,2048]{1,0:T(8,128)(2,1)} %x_hbm.1, f32[300,2048]{1,0:T(8,128)} %bitcast.6, f32[300,4096]{1,0:T(8,128)} %bitcast.5, f32[1,2048]{1,0:T(1,128)} %bitcast.7), custom_call_target="tpu_custom_call" | custom-call | tf_op jit(solution)/shard_map/pallas_call | solution.py:365
  335.0 8.4 %shard_map.60 = (f32[300,2048]{1,0:T(8,128)}, f32[300,4096]{1,0:T(8,128)}) custom-call(f32[304,2048]{1,0:T(8,128)} %get-tuple-element.6.w_in, f32[304,4096]{1,0:T(8,128)} %get-tuple-element.7.r_in), custom_call_target="tpu_custom_call" | custom-call | tf_op jit(solution)/shard_map/pallas_call | solution.py:386

commit v3 on v2

--- a/solution.py
+++ b/solution.py
@@ -12,7 +12,10 @@
 MIX_WEIGHT = 0.75
 CORES = 2
 ROW_TILE = 16
-PIECES = 2
+PIECES = 5
+TURN = 32
+RUNS = (7, 6, 4, 1, 1, 1, 1, 1, 1, 2, 3, 2, 2, 1, 2, 3, 4, 3, 2, 4, 2, 1, 3, 2,
+        1, 5, 4, 1, 1, 3, 2, 2, 3, 1, 1, 2, 1, 5, 4, 1, 2, 5, 5, 1, 1, 4)
 MESH = pl.DeviceIdType.MESH
 
 
@@ -26,8 +29,35 @@
     return tuple((r, min(size, rows - r)) for r in range(0, rows, size))
 
 
+def sweep_steps(far, pieces):
+    steps = []
+    for t in range(1, far + 1):
+        steps += [("send", t, p) for p in pieces]
+        v = far - t
+        steps += [("product", u, 0) for u in ((v, -v) if v else (0,))]
+    steps += [("finish", 0, p) for p in pieces]
+    for t in range(1, far + 1):
+        steps += [("gather", t, p) for p in pieces]
+        steps += [("gradient", t - 1, 0)]
+    return steps + [("update", 0, 0)]
+
+
+def schedule(group, far):
+    lists = []
+    for h, s in enumerate(group):
+        steps = [(s,) + step for step in sweep_steps(far, s.pieces)]
+        turn = TURN if h else len(steps)
+        lists.append([step + (1,) for step in steps[turn:]] + [step + (0,) for step in steps[:turn]])
+    order, h = [], 0
+    for run in RUNS:
+        order += lists[h][:run]
+        del lists[h][:run]
+        h = 1 - h
+    return order + lists[0] + lists[1]
+
+
 def kernel(chips, samples, streams, x_hbm, w_hbm, y_hbm, eta_ref, wout_hbm, rout_hbm,
-           x, wraw, yraw, w, res, grad, op, xsem, wsem, ysem, wosem, *rest):
+           x, wraw, yraw, w, res, grad, op, xsem, wsem, ysem, *rest):
     per = len(rest) // len(streams)
     st = [rest[i * per:(i + 1) * per] for i in range(len(streams))]
     far, near = chips // 2, chips - 1 - chips // 2
@@ -67,7 +97,7 @@
             self.pieces = range(len(self.cuts))
             (self.pbuf, self.precv, self.rp, self.rq, self.rbf, self.rfin,
              self.pd_s, self.pd_r, self.rsp_s, self.rsp_r, self.rsq_s, self.rsq_r,
-             self.agp_s, self.agp_r, self.agq_s, self.agq_r, self.agd_s, self.agd_r, self.osem) = st[index]
+             self.agp_s, self.agp_r, self.agq_s, self.agq_r, self.agd_s, self.agd_r, self.osem, self.wosem) = st[index]
 
         def ps(self, p):
             return pl.ds(*self.cuts[p])
@@ -234,6 +264,9 @@
             if real % ROW_TILE:
                 move(pl.ds(self.r0 + real // ROW_TILE * ROW_TILE, real % ROW_TILE))
 
+        def write_w(self):
+            return pltpu.make_async_copy(w.at[self.rs, :], wout_hbm.at[self.rs, :], self.wosem)
+
         def write(self, u, core):
             return pltpu.make_async_copy(self.rfin.at[u % chips, core],
                                          rout_hbm.at[self.rs, pl.ds(pl.multiple_of((chip_at(-u) * CORES + core) * block, block), block)],
@@ -265,69 +298,92 @@
     y_copy.wait()
     res[pl.ds(0, yraw.shape[0]), :] = yraw[...]
 
-    @pl.loop(0, SWEEPS + 1)
-    def _(it):
-        def products(s, vs):
-            for v in vs:
-                if s is group[0]:
-                    @pl.when(it == 0)
-                    def _():
-                        x_copy(v).wait()
-                s.product(v)
-
-        for t in range(1, far + 1):
-            v = far - t
-            vs = (v, -v) if v else (0,)
-            for s in group:
-                for p in s.pieces:
-                    s.pass_on(t, p)
-                products(s, vs)
-        for s in group:
-            for p in s.pieces:
-                s.finish(it, p)
-        for s in group:
-            s.settle_sums()
-
-        @pl.when(it < SWEEPS)
-        def _():
-            for t in range(1, far + 1):
-                for s in group:
-                    for p in s.pieces:
-                        s.ag_step(s.rbf, t, p)
-                    s.gradient(t - 1)
-                    if t == far:
-                        s.gradient(far)
-                        s.step()
-                        s.settle_gather(s.rbf)
-                        s.product(far)
-
-    w_out = pltpu.make_async_copy(w, wout_hbm, wosem)
-    w_out.start()
-
     def write_in(s, u):
         for p in s.pieces:
             s.ag_d_in(s.rfin, u, p).wait_recv()
         s.write(u, other).start()
 
+    def sum_step(s, kind, a, p, it, loads):
+        if kind == "send":
+            s.pass_on(a, p)
+        elif kind == "finish":
+            s.finish(it, p)
+        else:
+            if (s, a) in loads:
+                @pl.when(it == 0)
+                def _():
+                    x_copy(a).wait()
+            s.product(a)
+
+    def gather_step(s, kind, a, p, it):
+        if kind == "gather":
+            s.ag_step(s.rbf, a, p)
+        elif kind == "gradient":
+            s.gradient(a)
+        else:
+            s.gradient(far)
+            s.step()
+            s.settle_sums()
+            s.settle_gather(s.rbf)
+            s.product(far)
+
+            @pl.when(it == SWEEPS - 1)
+            def _():
+                s.write_w().start()
+
+    def last_step(s, kind, a, p):
+        if kind == "gather":
+            s.ag_step(s.rfin, a, p)
+        elif kind == "gradient":
+            for u in ((0,) if a == 0 else (a, -a)):
+                s.write(u, c).start()
+                write_in(s, u)
+        else:
+            s.write(far, c).start()
+            write_in(s, far)
+
+    steps = schedule(group, far)
+    lag = max(step[-1] for step in steps)
+    loads, seen = set(), set()
+    for j in range(lag + 1):
+        for s, kind, a, _, stage in steps:
+            if kind == "product" and j == stage and a not in seen:
+                seen.add(a)
+                loads.add((s, a))
+    batches = []
+    for step in steps:
+        key = (step[1] in ("send", "product", "finish"), step[-1])
+        if not batches or batches[-1][0] != key:
+            batches.append((key, []))
+        batches[-1][1].append(step[:-1])
+
+    @pl.loop(0, SWEEPS + 1 + lag)
+    def _(j):
+        for (sums, stage), batch in batches:
+            it = j - stage
+            if sums:
+                @pl.when((it >= 0) & (it <= SWEEPS))
+                def _():
+                    for step in batch:
+                        sum_step(*step, it, loads)
+            else:
+                @pl.when((it >= 0) & (it < SWEEPS))
+                def _():
+                    for step in batch:
+                        gather_step(*step, it)
+
+                @pl.when(it == SWEEPS)
+                def _():
+                    for step in batch:
+                        last_step(*step)
+
     for s in group:
-        s.write(0, c).start()
-    for t in range(1, far + 1):
-        for s in group:
-            for p in s.pieces:
-                s.ag_step(s.rfin, t, p)
-            s.write(t, c).start()
-            if t <= near:
-                s.write(-t, c).start()
-            for u in ((0,) if t == 1 else (t - 1, 1 - t)):
-                write_in(s, u)
-    for s in group:
-        write_in(s, far)
-    for s in group:
+        s.settle_sums()
         s.settle_gather(s.rfin)
         for u in range(chips):
             for core in (c, other):
                 s.write(u, core).wait()
-    w_out.wait()
+        s.write_w().wait()
 
 
 def solve(chips, design, w_t, y_t, eta):
@@ -346,7 +402,7 @@
         pltpu.VMEM((padded, block), f32),
         pltpu.VMEM((padded, depth), f32),
         pltpu.VMEM((padded, depth), bf16),
-        dma((chips,)), dma, dma, dma,
+        dma((chips,)), dma, dma,
     ]
     for _, rows in streams:
         scratch += [
@@ -359,7 +415,7 @@
             dma((chips,)), dma((chips,)),
             *[dma((hops, PIECES)) for hops in (far, far, near, near) * 2],
             dma((chips, PIECES)), dma((chips, PIECES)),
-            dma((chips, CORES)),
+            dma((chips, CORES)), dma,
         ]
     any_spec = pl.BlockSpec(memory_space=pl.ANY)
     return pl.pallas_call(

time: 344 us -> 330 us (0.959)
  Pallas kernels: 343 us -> 330 us
    pallas_call x1, Pallas kernels: 334 us -> 321 us  [solve(): pl.pallas_call(functools.partial(kernel, chips, samples, streams), out_sh...]
where the time goes in v3:
time: 330 us
  Pallas kernels  330 us (100%)
    pallas_call x1, Pallas kernels, solve(): pl.pallas_call(functools.partial(kernel, chips, samples, streams), out_sh...  321 us
    pallas_call x1, Pallas kernels, trim(): pl.pallas_call(functools.partial(trim_kernel, k), out_shape=tuple((jax.Sh...  8.39 us

profile of v3, /device:TPU:21, one launch (start us, length us, event | category | flops | bytes accessed | tf_op | source)
XLA Modules:
  0.0 330.2 jit_solution(8369030998280362207)
XLA Ops:
  0.6 321.1 %shard_map.59 = (f32[304,2048]{1,0:T(8,128)}, f32[304,4096]{1,0:T(8,128)}) custom-call(bf16[4096,2048]{1,0:T(8,128)(2,1)} %x_hbm.1, f32[300,2048]{1,0:T(8,128)} %bitcast.6, f32[300,4096]{1,0:T(8,128)} %bitcast.5, f32[1,2048]{1,0:T(1,128)} %bitcast.7), custom_call_target="tpu_custom_call" | custom-call | tf_op jit(solution)/shard_map/pallas_call | solution.py:421
  321.8 8.4 %shard_map.60 = (f32[300,2048]{1,0:T(8,128)}, f32[300,4096]{1,0:T(8,128)}) custom-call(f32[304,2048]{1,0:T(8,128)} %get-tuple-element.6.w_in, f32[304,4096]{1,0:T(8,128)} %get-tuple-element.7.r_in), custom_call_target="tpu_custom_call" | custom-call | tf_op jit(solution)/shard_map/pallas_call | solution.py:442

commit v4 on v3

--- a/solution.py
+++ b/solution.py
@@ -12,16 +12,24 @@
 MIX_WEIGHT = 0.75
 CORES = 2
 ROW_TILE = 16
-PIECES = 5
-TURN = 32
-RUNS = (7, 6, 4, 1, 1, 1, 1, 1, 1, 2, 3, 2, 2, 1, 2, 3, 4, 3, 2, 4, 2, 1, 3, 2,
-        1, 5, 4, 1, 1, 3, 2, 2, 3, 1, 1, 2, 1, 5, 4, 1, 2, 5, 5, 1, 1, 4)
+PIECES = 2
+TILES = (7, 6, 6)
+TURNS = (None, 26, 17)
+RUNS = (
+    (0, 4), (2, 2), (1, 1), (2, 1), (1, 2), (0, 2), (1, 1), (2, 1), (0, 2), (2, 1), (1, 3),
+    (2, 1), (0, 1), (1, 1), (0, 1), (2, 1), (0, 2), (2, 2), (1, 2), (0, 1), (1, 2), (2, 1),
+    (0, 2), (2, 2), (1, 1), (2, 1), (1, 3), (0, 1), (2, 1), (0, 1), (2, 3), (1, 3), (0, 2),
+    (2, 3), (1, 2), (2, 1), (0, 3), (2, 2), (1, 1), (2, 2), (1, 1), (0, 3), (1, 1), (2, 1),
+    (0, 1), (2, 2), (1, 1), (0, 1), (1, 1), (0, 1), (1, 1), (0, 1), (2, 1), (0, 1), (2, 1),
+    (1, 3),
+)
 MESH = pl.DeviceIdType.MESH
 
 
 def split_rows(padded):
-    first = -(-padded // (2 * ROW_TILE)) * ROW_TILE
-    return ((0, first), (first, padded - first))
+    sizes = [tiles * ROW_TILE for tiles in TILES]
+    assert sum(sizes) == padded
+    return tuple((sum(sizes[:i]), size) for i, size in enumerate(sizes))
 
 
 def split_pieces(rows):
@@ -46,14 +54,14 @@
     lists = []
     for h, s in enumerate(group):
         steps = [(s,) + step for step in sweep_steps(far, s.pieces)]
-        turn = TURN if h else len(steps)
+        turn = len(steps) if TURNS[h] is None else TURNS[h]
         lists.append([step + (1,) for step in steps[turn:]] + [step + (0,) for step in steps[:turn]])
-    order, h = [], 0
-    for run in RUNS:
+    order = []
+    for h, run in RUNS:
         order += lists[h][:run]
         del lists[h][:run]
-        h = 1 - h
-    return order + lists[0] + lists[1]
+    assert not any(lists)
+    return order
 
 
 def kernel(chips, samples, streams, x_hbm, w_hbm, y_hbm, eta_ref, wout_hbm, rout_hbm,
@@ -126,13 +134,13 @@
             return remote(buf.at[-(t - 1) % chips, c, ps], buf.at[-t % chips, c, ps], self.agq_s.at[t - 1, p],
                           self.agq_r.at[t - 1, p], nbr_q)
 
-        def ag_d(self, buf, u, p):
-            a, b, ps = u % chips, -u % chips, self.ps(p)
-            return remote(buf.at[a, c, ps], buf.at[b, c, ps], self.agd_s.at[a, p], self.agd_r.at[b, p], sib)
-
-        def ag_d_in(self, buf, u, p):
-            a, ps = u % chips, self.ps(p)
-            return remote(buf.at[a, other, ps], buf.at[a, other, ps], self.agd_s.at[a, p], self.agd_r.at[a, p], sib)
+        def ag_d(self, buf, u):
+            a, b = u % chips, -u % chips
+            return remote(buf.at[a, c], buf.at[b, c], self.agd_s.at[a], self.agd_r.at[b], sib)
+
+        def ag_d_in(self, buf, u):
+            a = u % chips
+            return remote(buf.at[a, other], buf.at[a, other], self.agd_s.at[a], self.agd_r.at[a], sib)
 
         def product(self, v):
             out = lax.dot_general(op[self.rs, :], x[x_rows(v), :], (((1,), (1,)), ((), ())),
@@ -192,18 +200,21 @@
         def ag_open(self, buf, p):
             self.ag_p(buf, 1, p).start()
             self.ag_q(buf, 1, p).start()
-            self.ag_d(buf, 0, p).start()
+            if p == self.pieces[-1]:
+                self.ag_d(buf, 0).start()
 
         def ag_step(self, buf, t, p):
             self.ag_p(buf, t, p).wait_recv()
             if t < far:
                 self.ag_p(buf, t + 1, p).start()
-            self.ag_d(buf, t, p).start()
+            if p == self.pieces[-1]:
+                self.ag_d(buf, t).start()
             if t <= near:
                 self.ag_q(buf, t, p).wait_recv()
                 if t < near:
                     self.ag_q(buf, t + 1, p).start()
-                self.ag_d(buf, -t, p).start()
+                if p == self.pieces[-1]:
+                    self.ag_d(buf, -t).start()
 
         def settle_sums(self):
             for v in range(chips):
@@ -220,15 +231,14 @@
                     self.ag_p(buf, t, p).wait_send()
                 for t in range(1, near + 1):
                     self.ag_q(buf, t, p).wait_send()
-                for u in range(chips):
-                    self.ag_d(buf, u, p).wait_send()
+            for u in range(chips):
+                self.ag_d(buf, u).wait_send()
 
         def gradient(self, t):
             offsets = (t, -t) if 0 < t <= near else (t,)
             parts = []
             for u in offsets:
-                for p in self.pieces:
-                    self.ag_d_in(self.rbf, u, p).wait_recv()
+                self.ag_d_in(self.rbf, u).wait_recv()
                 parts.append((jnp.concatenate([self.rbf[u % chips, core] for core in range(CORES)], axis=1), x_rows(-u)))
             wide = min(depth, 1024)
             for j in range(depth // wide):
@@ -299,8 +309,7 @@
     res[pl.ds(0, yraw.shape[0]), :] = yraw[...]
 
     def write_in(s, u):
-        for p in s.pieces:
-            s.ag_d_in(s.rfin, u, p).wait_recv()
+        s.ag_d_in(s.rfin, u).wait_recv()
         s.write(u, other).start()
 
     def sum_step(s, kind, a, p, it, loads):
@@ -414,7 +423,7 @@
             pltpu.VMEM((chips, CORES, rows, block), f32),
             dma((chips,)), dma((chips,)),
             *[dma((hops, PIECES)) for hops in (far, far, near, near) * 2],
-            dma((chips, PIECES)), dma((chips, PIECES)),
+            dma((chips,)), dma((chips,)),
             dma((chips, CORES)), dma,
         ]
     any_spec = pl.BlockSpec(memory_space=pl.ANY)
@@ -430,21 +439,44 @@
     )(design, w_t, y_t, eta)
 
 
-def trim_kernel(k, w_in, r_in, w_out, r_out):
-    w_out[...] = w_in[:k, :]
-    r_out[...] = r_in[:k, :]
+def trim_kernel(steps, w_in, r_in, w_out, r_out, w_a, w_b, r_a, r_b, isem, osem):
+    arrays = ((w_in, w_a, w_b, w_out), (r_in, r_a, r_b, r_out))
+
+    def fetch(n, i):
+        src, a, _, _ = arrays[n]
+        return pltpu.make_async_copy(src.at[:, pl.ds(i * a.shape[2], a.shape[2])], a.at[i], isem.at[n, i])
+
+    def store(n, i):
+        _, _, b, dst = arrays[n]
+        return pltpu.make_async_copy(b.at[i], dst.at[:, pl.ds(i * b.shape[2], b.shape[2])], osem.at[n, i])
+
+    every = [(n, i) for i in range(steps) for n in range(len(arrays))]
+    for n, i in every:
+        fetch(n, i).start()
+    for n, i in every:
+        fetch(n, i).wait()
+        _, a, b, _ = arrays[n]
+        b[i] = a[i, :b.shape[1], :]
+        store(n, i).start()
+    for n, i in every:
+        store(n, i).wait()
 
 
 def trim(k, steps, w_t, r_t):
-    def spec(rows, arr):
-        return pl.BlockSpec((rows, arr.shape[1] // steps), lambda i: (0, i))
-
+    any_spec = pl.BlockSpec(memory_space=pltpu.HBM)
+    arrays = (w_t, r_t)
     return pl.pallas_call(
-        functools.partial(trim_kernel, k),
-        out_shape=tuple(jax.ShapeDtypeStruct((k, a.shape[1]), a.dtype) for a in (w_t, r_t)),
-        grid=(steps,),
-        in_specs=[spec(a.shape[0], a) for a in (w_t, r_t)],
-        out_specs=tuple(spec(k, a) for a in (w_t, r_t)),
+        functools.partial(trim_kernel, steps),
+        out_shape=tuple(jax.ShapeDtypeStruct((k, a.shape[1]), a.dtype) for a in arrays),
+        in_specs=[any_spec, any_spec],
+        out_specs=(any_spec, any_spec),
+        scratch_shapes=[
+            *[pltpu.VMEM((steps, rows, a.shape[1] // steps), a.dtype)
+              for a in arrays for rows in (a.shape[0], k)],
+            pltpu.SemaphoreType.DMA((2, steps)),
+            pltpu.SemaphoreType.DMA((2, steps)),
+        ],
+        compiler_params=pltpu.CompilerParams(vmem_limit_bytes=60 * 1024 * 1024),
     )(w_t, r_t)
 
 

time: 330 us -> 335 us (1.015)
  Pallas kernels: 330 us -> 334 us
    pallas_call x1, Pallas kernels: 321 us -> 328 us  [solve(): pl.pallas_call(functools.partial(kernel, chips, samples, streams), out_sh...]
where the time goes in v4:
time: 335 us
  Pallas kernels  334 us (100%)
    pallas_call x1, Pallas kernels, solve(): pl.pallas_call(functools.partial(kernel, chips, samples, streams), out_sh...  328 us

profile of v4, /device:TPU:21, one launch (start us, length us, event | category | flops | bytes accessed | tf_op | source)
XLA Modules:
  0.0 334.8 jit_solution(4232065189701947567)
XLA Ops:
  0.6 328.1 %shard_map.59 = (f32[304,2048]{1,0:T(8,128)}, f32[304,4096]{1,0:T(8,128)}) custom-call(bf16[4096,2048]{1,0:T(8,128)(2,1)} %x_hbm.1, f32[300,2048]{1,0:T(8,128)} %bitcast.6, f32[300,4096]{1,0:T(8,128)} %bitcast.5, f32[1,2048]{1,0:T(1,128)} %bitcast.7), custom_call_target="tpu_custom_call" | custom-call | tf_op jit(solution)/shard_map/pallas_call | solution.py:430
  328.7 6.1 %shard_map.60 = (f32[300,2048]{1,0:T(8,128)}, f32[300,4096]{1,0:T(8,128)}) custom-call(f32[304,2048]{1,0:T(8,128)} %get-tuple-element.6.w_in, f32[304,4096]{1,0:T(8,128)} %get-tuple-element.7.r_in), custom_call_target="tpu_custom_call" | custom-call | tf_op jit(solution)/shard_map/pallas_call | solution.py:468

commit v5 on v4

--- a/solution.py
+++ b/solution.py
@@ -12,16 +12,13 @@
 MIX_WEIGHT = 0.75
 CORES = 2
 ROW_TILE = 16
-PIECES = 2
-TILES = (7, 6, 6)
-TURNS = (None, 26, 17)
+PIECES = 3
+TILES = (10, 9)
+TURNS = (None, 22)
 RUNS = (
-    (0, 4), (2, 2), (1, 1), (2, 1), (1, 2), (0, 2), (1, 1), (2, 1), (0, 2), (2, 1), (1, 3),
-    (2, 1), (0, 1), (1, 1), (0, 1), (2, 1), (0, 2), (2, 2), (1, 2), (0, 1), (1, 2), (2, 1),
-    (0, 2), (2, 2), (1, 1), (2, 1), (1, 3), (0, 1), (2, 1), (0, 1), (2, 3), (1, 3), (0, 2),
-    (2, 3), (1, 2), (2, 1), (0, 3), (2, 2), (1, 1), (2, 2), (1, 1), (0, 3), (1, 1), (2, 1),
-    (0, 1), (2, 2), (1, 1), (0, 1), (1, 1), (0, 1), (1, 1), (0, 1), (2, 1), (0, 1), (2, 1),
-    (1, 3),
+    (0, 5), (1, 4), (0, 2), (1, 1), (0, 1), (1, 1), (0, 2), (1, 1), (0, 1), (1, 1), (0, 4),
+    (1, 4), (0, 4), (1, 4), (0, 1), (1, 1), (0, 3), (1, 5), (0, 4), (1, 5), (0, 2), (1, 1),
+    (0, 1), (1, 3), (0, 3), (1, 1), (0, 1), (1, 4), (0, 5), (1, 3),
 )
 MESH = pl.DeviceIdType.MESH
 
@@ -288,22 +285,23 @@
     w_copy = pltpu.make_async_copy(w_hbm, wraw, wsem)
     w_copy.start()
     x_copy(far).start()
-    for v in order[1:]:
-        x_copy(v).start()
     mine = pl.ds(pl.multiple_of(feat * block, block), block)
     y_copy = pltpu.make_async_copy(y_hbm.at[:, mine], yraw, ysem)
-    y_copy.start()
 
     barrier = pltpu.get_barrier_semaphore()
     for dev in (sib, nbr_p, nbr_q):
         pl.semaphore_signal(barrier, inc=1, device_id=dev, device_id_type=MESH)
+
+    w_copy.wait()
+    for v in order[1:]:
+        x_copy(v).start()
+    y_copy.start()
+    group[0].cast()
+    x_copy(far).wait()
     pl.semaphore_wait(barrier, 3)
-
-    w_copy.wait()
-    for s in group:
+    group[0].product(far)
+    for s in group[1:]:
         s.cast()
-    x_copy(far).wait()
-    for s in group:
         s.product(far)
     y_copy.wait()
     res[pl.ds(0, yraw.shape[0]), :] = yraw[...]

time: 335 us -> 331 us (0.988)
  Pallas kernels: 334 us -> 330 us
    pallas_call x1, Pallas kernels: 328 us -> 324 us  [solve(): pl.pallas_call(functools.partial(kernel, chips, samples, streams), out_sh...]
where the time goes in v5:
time: 331 us
  Pallas kernels  330 us (100%)
    pallas_call x1, Pallas kernels, solve(): pl.pallas_call(functools.partial(kernel, chips, samples, streams), out_sh...  324 us

profile of v5, /device:TPU:21, one launch (start us, length us, event | category | flops | bytes accessed | tf_op | source)
XLA Modules:
  0.0 330.7 jit_solution(9821461731122080427)
XLA Ops:
  0.6 323.9 %shard_map.59 = (f32[304,2048]{1,0:T(8,128)}, f32[304,4096]{1,0:T(8,128)}) custom-call(bf16[4096,2048]{1,0:T(8,128)(2,1)} %x_hbm.1, f32[300,2048]{1,0:T(8,128)} %bitcast.6, f32[300,4096]{1,0:T(8,128)} %bitcast.5, f32[1,2048]{1,0:T(1,128)} %bitcast.7), custom_call_target="tpu_custom_call" | custom-call | tf_op jit(solution)/shard_map/pallas_call | solution.py:428
  324.6 6.1 %shard_map.60 = (f32[300,2048]{1,0:T(8,128)}, f32[300,4096]{1,0:T(8,128)}) custom-call(f32[304,2048]{1,0:T(8,128)} %get-tuple-element.6.w_in, f32[304,4096]{1,0:T(8,128)} %get-tuple-element.7.r_in), custom_call_target="tpu_custom_call" | custom-call | tf_op jit(solution)/shard_map/pallas_call | solution.py:466

commit v6 on v3

--- a/solution.py
+++ b/solution.py
@@ -278,22 +278,23 @@
     w_copy = pltpu.make_async_copy(w_hbm, wraw, wsem)
     w_copy.start()
     x_copy(far).start()
-    for v in order[1:]:
-        x_copy(v).start()
     mine = pl.ds(pl.multiple_of(feat * block, block), block)
     y_copy = pltpu.make_async_copy(y_hbm.at[:, mine], yraw, ysem)
-    y_copy.start()
 
     barrier = pltpu.get_barrier_semaphore()
     for dev in (sib, nbr_p, nbr_q):
         pl.semaphore_signal(barrier, inc=1, device_id=dev, device_id_type=MESH)
+
+    w_copy.wait()
+    for v in order[1:]:
+        x_copy(v).start()
+    y_copy.start()
+    group[0].cast()
+    x_copy(far).wait()
     pl.semaphore_wait(barrier, 3)
-
-    w_copy.wait()
-    for s in group:
+    group[0].product(far)
+    for s in group[1:]:
         s.cast()
-    x_copy(far).wait()
-    for s in group:
         s.product(far)
     y_copy.wait()
     res[pl.ds(0, yraw.shape[0]), :] = yraw[...]
@@ -430,21 +431,44 @@
     )(design, w_t, y_t, eta)
 
 
-def trim_kernel(k, w_in, r_in, w_out, r_out):
-    w_out[...] = w_in[:k, :]
-    r_out[...] = r_in[:k, :]
+def trim_kernel(steps, w_in, r_in, w_out, r_out, w_a, w_b, r_a, r_b, isem, osem):
+    arrays = ((w_in, w_a, w_b, w_out), (r_in, r_a, r_b, r_out))
+
+    def fetch(n, i):
+        src, a, _, _ = arrays[n]
+        return pltpu.make_async_copy(src.at[:, pl.ds(i * a.shape[2], a.shape[2])], a.at[i], isem.at[n, i])
+
+    def store(n, i):
+        _, _, b, dst = arrays[n]
+        return pltpu.make_async_copy(b.at[i], dst.at[:, pl.ds(i * b.shape[2], b.shape[2])], osem.at[n, i])
+
+    every = [(n, i) for i in range(steps) for n in range(len(arrays))]
+    for n, i in every:
+        fetch(n, i).start()
+    for n, i in every:
+        fetch(n, i).wait()
+        _, a, b, _ = arrays[n]
+        b[i] = a[i, :b.shape[1], :]
+        store(n, i).start()
+    for n, i in every:
+        store(n, i).wait()
 
 
 def trim(k, steps, w_t, r_t):
-    def spec(rows, arr):
-        return pl.BlockSpec((rows, arr.shape[1] // steps), lambda i: (0, i))
-
+    any_spec = pl.BlockSpec(memory_space=pltpu.HBM)
+    arrays = (w_t, r_t)
     return pl.pallas_call(
-        functools.partial(trim_kernel, k),
-        out_shape=tuple(jax.ShapeDtypeStruct((k, a.shape[1]), a.dtype) for a in (w_t, r_t)),
-        grid=(steps,),
-        in_specs=[spec(a.shape[0], a) for a in (w_t, r_t)],
-        out_specs=tuple(spec(k, a) for a in (w_t, r_t)),
+        functools.partial(trim_kernel, steps),
+        out_shape=tuple(jax.ShapeDtypeStruct((k, a.shape[1]), a.dtype) for a in arrays),
+        in_specs=[any_spec, any_spec],
+        out_specs=(any_spec, any_spec),
+        scratch_shapes=[
+            *[pltpu.VMEM((steps, rows, a.shape[1] // steps), a.dtype)
+              for a in arrays for rows in (a.shape[0], k)],
+            pltpu.SemaphoreType.DMA((2, steps)),
+            pltpu.SemaphoreType.DMA((2, steps)),
+        ],
+        compiler_params=pltpu.CompilerParams(vmem_limit_bytes=60 * 1024 * 1024),
     )(w_t, r_t)
 
 

time: 330 us -> 329 us (level)
  no operation moved by 1% of the time
where the time goes in v6:
time: 329 us
  Pallas kernels  329 us (100%)
    pallas_call x1, Pallas kernels, solve(): pl.pallas_call(functools.partial(kernel, chips, samples, streams), out_sh...  322 us

profile of v6, /device:TPU:21, one launch (start us, length us, event | category | flops | bytes accessed | tf_op | source)
XLA Modules:
  0.0 329.2 jit_solution(3765210456165573180)
XLA Ops:
  0.6 322.4 %shard_map.59 = (f32[304,2048]{1,0:T(8,128)}, f32[304,4096]{1,0:T(8,128)}) custom-call(bf16[4096,2048]{1,0:T(8,128)(2,1)} %x_hbm.1, f32[300,2048]{1,0:T(8,128)} %bitcast.6, f32[300,4096]{1,0:T(8,128)} %bitcast.5, f32[1,2048]{1,0:T(1,128)} %bitcast.7), custom_call_target="tpu_custom_call" | custom-call | tf_op jit(solution)/shard_map/pallas_call | solution.py:422
  323.1 6.1 %shard_map.60 = (f32[300,2048]{1,0:T(8,128)}, f32[300,4096]{1,0:T(8,128)}) custom-call(f32[304,2048]{1,0:T(8,128)} %get-tuple-element.6.w_in, f32[304,4096]{1,0:T(8,128)} %get-tuple-element.7.r_in), custom_call_target="tpu_custom_call" | custom-call | tf_op jit(solution)/shard_map/pallas_call | solution.py:460
